TPU v7x, 32 devices: a whole 2x2x4 slice. The times are simulated.
32 devices in a mesh: dp: 16 (over z, y, x), mp: 2 (over core).
Axes of the slice: x: 2, y: 2, z: 4, core: 2. Of those that a mesh axis runs over, the one named last changes fastest.
Arguments:
- hidden_state: bfloat16 [32, 19, 19, 256], P('dp'), may hold values from -6 to 6
- actions: int32 [32, 2], P('dp'), may hold values from 0 to 361
- value_target: int32 [32, 2], P('dp'), may hold values from 0 to 600
- reward_target: int32 [32, 2], P('dp'), may hold values from 0 to 600
- kernel_first: float32 [3, 3, 256, 256], P(None, None, 'dp', 'mp'), may hold values from -6 to 6
- kernel_second: float32 [3, 3, 256, 256], P(None, None, 'dp', 'mp'), may hold values from -6 to 6
- head_weight: float32 [2, 256, 601], P('mp', 'dp'), may hold values from -6 to 6
- action_embed: float32 [2, 256], P('mp', 'dp'), may hold values from -6 to 6
- first_mean: float32 [3, 3, 256, 256], P(None, None, 'dp', 'mp'), may hold values from -0.00061035156 to 0.00061035156
- first_square: float32 [3, 3, 256, 256], P(None, None, 'dp', 'mp'), may hold values from 1e-09 to 1e-06
- second_mean: float32 [3, 3, 256, 256], P(None, None, 'dp', 'mp'), may hold values from -0.00061035156 to 0.00061035156
- second_square: float32 [3, 3, 256, 256], P(None, None, 'dp', 'mp'), may hold values from 1e-09 to 1e-06
- head_mean: float32 [2, 256, 601], P('mp', 'dp'), may hold values from -0.0029296875 to 0.0029296875
- head_square: float32 [2, 256, 601], P('mp', 'dp'), may hold values from 1e-08 to 1e-06
- embed_mean: float32 [2, 256], P('mp', 'dp'), may hold values from -0.0017089844 to 0.0017089844
- embed_square: float32 [2, 256], P('mp', 'dp'), may hold values from 1e-09 to 1e-06
Outputs:
- kernel_first_new: float32 [3, 3, 256, 256], P(None, None, 'dp', 'mp')
- kernel_second_new: float32 [3, 3, 256, 256], P(None, None, 'dp', 'mp')
- head_weight_new: float32 [2, 256, 601], P('mp', 'dp')
- action_embed_new: float32 [2, 256], P('mp', 'dp')
- first_mean_new: float32 [3, 3, 256, 256], P(None, None, 'dp', 'mp')
- first_square_new: float32 [3, 3, 256, 256], P(None, None, 'dp', 'mp')
- second_mean_new: float32 [3, 3, 256, 256], P(None, None, 'dp', 'mp')
- second_square_new: float32 [3, 3, 256, 256], P(None, None, 'dp', 'mp')
- head_mean_new: float32 [2, 256, 601], P('mp', 'dp')
- head_square_new: float32 [2, 256, 601], P('mp', 'dp')
- embed_mean_new: float32 [2, 256], P('mp', 'dp')
- embed_square_new: float32 [2, 256], P('mp', 'dp')
- first_grad: float32 [3, 3, 256, 256], P(None, None, 'dp', 'mp')
- second_grad: float32 [3, 3, 256, 256], P(None, None, 'dp', 'mp')
- head_grad: float32 [2, 256, 601], P('mp', 'dp')
- embed_grad: float32 [2, 256], P('mp', 'dp')
Inputs may be any that keep to these rules, and one draw needn't show every extreme that they name: `actions`: the value 361 stands for a pass.
All inputs are finite; a program needn't handle non-finite values.
Results may differ from a plain program's by a relative error of at most 0.02.
Values may be sent and summed in bfloat16 or wider, within the bound.
No kernel may reach another device: no remote copies, remote signals or barrier semaphores. Data moves between devices by JAX's collectives and lax.ppermute only.
A program may use at most 64 MiB of HBM per device.

v0:
```python
import jax
import jax.numpy as jnp
from jax import lax
from jax.sharding import PartitionSpec as P

CHANNELS = 256


head_scale = 4.0
soft_cap = 15.0
eps_norm = 1e-05
beta_one = 0.9
beta_two = 0.999
step_size = 0.1
eps_adam = 1e-08


def conv_apply(field, kernel, layout):
    return lax.conv_general_dilated(
        field,
        kernel,
        (1, 1),
        "SAME",
        dimension_numbers=("NHWC", layout, "NHWC"),
        preferred_element_type=jnp.float32,
    )


def gate_slope(pre):
    sig = jax.nn.sigmoid(pre)
    return sig * (1.0 + pre * (1.0 - sig))


def tap_products(field, grad, field_rows):
    side = field.shape[1]
    padded = jnp.pad(field, ((0, 0), (1, 1), (1, 1), (0, 0)))
    flat_grad = grad.reshape(-1, grad.shape[3])
    blocks = []
    for offset in range(9):
        row_start = offset // 3
        col_start = offset % 3
        window = padded[:, row_start : row_start + side, col_start : col_start + side, :].reshape(
            -1, field.shape[3]
        )
        if field_rows:
            blocks.append(
                lax.dot_general(
                    window, flat_grad, (((0,), (0,)), ((), ())), preferred_element_type=jnp.float32
                )
            )
        else:
            blocks.append(
                lax.dot_general(
                    flat_grad, window, (((0,), (0,)), ((), ())), preferred_element_type=jnp.float32
                )
            )
    stacked = jnp.stack(blocks)
    return stacked.reshape(3, 3, stacked.shape[1], stacked.shape[2])


def action_planes(move, board):
    cells = board * board
    plane = (lax.broadcasted_iota(jnp.int32, (move.shape[0], cells), 1) == move[:, None]).astype(
        jnp.float32
    )
    passed = (move == cells).astype(jnp.float32)
    return (plane.reshape(move.shape[0], board, board, 1), passed[:, None, None, None])


def head_backward(state, head_used, value_now, reward_now, total):
    pooled = jnp.mean(state, axis=(1, 2)).astype(jnp.bfloat16)
    raw = head_scale * jnp.stack(
        [
            jnp.dot(pooled, head_used[0], preferred_element_type=jnp.float32),
            jnp.dot(pooled, head_used[1], preferred_element_type=jnp.float32),
        ]
    )
    squashed = jnp.tanh(raw / soft_cap)
    raised = jnp.exp(soft_cap * squashed)
    chances = raised / jnp.sum(raised, axis=2, keepdims=True)
    targets = jnp.stack([value_now, reward_now])
    picked = (lax.broadcasted_iota(jnp.int32, raw.shape, 2) == targets[:, :, None]).astype(
        jnp.float32
    )
    logit_grad = ((chances - picked) * (1.0 - squashed * squashed) / total).astype(jnp.bfloat16)
    pooled_grad = head_scale * (
        jnp.dot(logit_grad[0], head_used[0].T, preferred_element_type=jnp.float32)
        + jnp.dot(logit_grad[1], head_used[1].T, preferred_element_type=jnp.float32)
    )
    return (pooled, logit_grad, pooled_grad)


def adam_update(param, grad, mean, square):
    mean_new = beta_one * mean + (1.0 - beta_one) * grad
    square_new = beta_two * square + (1.0 - beta_two) * grad * grad
    param_new = param - step_size * mean_new / (jnp.sqrt(square_new) + eps_adam)
    return (param_new, mean_new, square_new)


def local(
    hidden_state,
    actions,
    value_target,
    reward_target,
    kernel_first,
    kernel_second,
    head_weight,
    action_embed,
    first_mean,
    first_square,
    second_mean,
    second_square,
    head_mean,
    head_square,
    embed_mean,
    embed_square,
):
    total = hidden_state.shape[0] * lax.axis_size("dp")
    board = hidden_state.shape[1]
    cells = board * board
    scale = (9.0 * CHANNELS) ** (-0.5)
    first_used, second_used, head_used, embed_used = (
        lax.all_gather(kernel_first.astype(jnp.bfloat16), "dp", axis=2, tiled=True),
        lax.all_gather(kernel_second.astype(jnp.bfloat16), "dp", axis=2, tiled=True),
        lax.all_gather(head_weight.astype(jnp.bfloat16), "dp", axis=1, tiled=True),
        lax.all_gather(action_embed.astype(jnp.bfloat16), "dp", axis=1, tiled=True),
    )
    first_used, second_used, head_used, embed_used = (
        lax.all_gather(first_used, "mp", axis=3, tiled=True),
        lax.all_gather(second_used, "mp", axis=3, tiled=True),
        lax.all_gather(head_used, "mp", axis=0, tiled=True),
        lax.all_gather(embed_used, "mp", axis=0, tiled=True),
    )
    count = hidden_state.shape[0] // lax.axis_size("mp")
    begin = lax.axis_index("mp") * count
    states = lax.dynamic_slice_in_dim(hidden_state, begin, count, 0)
    moves = lax.dynamic_slice_in_dim(actions, begin, count, 0)
    values = lax.dynamic_slice_in_dim(value_target, begin, count, 0)
    rewards = lax.dynamic_slice_in_dim(reward_target, begin, count, 0)
    unroll = moves.shape[1]
    embed = embed_used.astype(jnp.float32)
    state = states.astype(jnp.float32)
    saved = []
    for position in range(unroll):
        plane, passed = action_planes(moves[:, position], board)
        mixed = state + plane * embed[0] + passed * embed[1]
        conv_input = mixed.astype(jnp.bfloat16)
        pre = scale * conv_apply(conv_input, first_used, "HWIO")
        hidden = jax.nn.silu(pre).astype(jnp.bfloat16)
        branch = conv_apply(hidden, second_used, "HWOI")
        summed = mixed + scale * branch
        factor = lax.rsqrt(jnp.mean(summed * summed, axis=(1, 2, 3), keepdims=True) + eps_norm)
        state = summed * factor
        pooled, logit_grad, pooled_grad = head_backward(
            state, head_used, values[:, position], rewards[:, position], total
        )
        saved.append(
            (
                plane,
                passed,
                conv_input,
                pre,
                hidden,
                summed,
                factor,
                pooled,
                logit_grad,
                pooled_grad,
            )
        )
    first_grad = jnp.zeros(first_used.shape, jnp.float32)
    second_grad = jnp.zeros(second_used.shape, jnp.float32)
    head_grad = jnp.zeros(head_used.shape, jnp.float32)
    embed_grad = jnp.zeros(embed_used.shape, jnp.float32)
    carry = jnp.zeros(states.shape, jnp.float32)
    for position in range(unroll - 1, -1, -1):
        plane, passed, conv_input, pre, hidden, summed, factor, pooled, logit_grad, pooled_grad = (
            saved[position]
        )
        state_grad = carry + pooled_grad[:, None, None, :] / cells
        summed_grad = factor * state_grad - factor * factor * factor * summed * jnp.mean(
            state_grad * summed, axis=(1, 2, 3), keepdims=True
        )
        branch_grad = summed_grad.astype(jnp.bfloat16)
        hidden_grad = scale * conv_apply(branch_grad, second_used[::-1, ::-1], "HWIO")
        inner_grad = (hidden_grad * gate_slope(pre)).astype(jnp.bfloat16)
        input_grad = conv_apply(inner_grad, first_used[::-1, ::-1], "HWOI")
        carry = summed_grad + scale * input_grad
        first_grad = first_grad + scale * tap_products(conv_input, inner_grad, True)
        second_grad = second_grad + scale * tap_products(hidden, branch_grad, False)
        head_grad = head_grad + head_scale * jnp.stack(
            [
                lax.dot_general(
                    pooled,
                    logit_grad[0],
                    (((0,), (0,)), ((), ())),
                    preferred_element_type=jnp.float32,
                ),
                lax.dot_general(
                    pooled,
                    logit_grad[1],
                    (((0,), (0,)), ((), ())),
                    preferred_element_type=jnp.float32,
                ),
            ]
        )
        embed_grad = embed_grad + jnp.stack(
            [jnp.sum(plane * carry, axis=(0, 1, 2)), jnp.sum(passed * carry, axis=(0, 1, 2))]
        )
    first_grad, second_grad, head_grad, embed_grad = (
        lax.psum_scatter(first_grad, "mp", scatter_dimension=3, tiled=True),
        lax.psum_scatter(second_grad, "mp", scatter_dimension=3, tiled=True),
        lax.psum_scatter(head_grad, "mp", scatter_dimension=0, tiled=True),
        lax.psum_scatter(embed_grad, "mp", scatter_dimension=0, tiled=True),
    )
    first_grad, second_grad, head_grad, embed_grad = (
        lax.psum_scatter(first_grad, "dp", scatter_dimension=2, tiled=True),
        lax.psum_scatter(second_grad, "dp", scatter_dimension=2, tiled=True),
        lax.psum_scatter(head_grad, "dp", scatter_dimension=1, tiled=True),
        lax.psum_scatter(embed_grad, "dp", scatter_dimension=1, tiled=True),
    )
    first_new, first_mean_new, first_square_new = adam_update(
        kernel_first, first_grad, first_mean, first_square
    )
    second_new, second_mean_new, second_square_new = adam_update(
        kernel_second, second_grad, second_mean, second_square
    )
    head_new, head_mean_new, head_square_new = adam_update(
        head_weight, head_grad, head_mean, head_square
    )
    embed_new, embed_mean_new, embed_square_new = adam_update(
        action_embed, embed_grad, embed_mean, embed_square
    )
    return (
        first_new,
        second_new,
        head_new,
        embed_new,
        first_mean_new,
        first_square_new,
        second_mean_new,
        second_square_new,
        head_mean_new,
        head_square_new,
        embed_mean_new,
        embed_square_new,
        first_grad,
        second_grad,
        head_grad,
        embed_grad,
    )


def solution(mesh):
    placed = (
        P("dp", None, None, None),
        P("dp", None),
        P("dp", None),
        P("dp", None),
        P(None, None, "dp", "mp"),
        P(None, None, "dp", "mp"),
        P("mp", "dp", None),
        P("mp", "dp"),
        P(None, None, "dp", "mp"),
        P(None, None, "dp", "mp"),
        P(None, None, "dp", "mp"),
        P(None, None, "dp", "mp"),
        P("mp", "dp", None),
        P("mp", "dp", None),
        P("mp", "dp"),
        P("mp", "dp"),
    )
    return jax.shard_map(
        local,
        mesh=mesh,
        in_specs=placed,
        out_specs=(
            P(None, None, "dp", "mp"),
            P(None, None, "dp", "mp"),
            P("mp", "dp", None),
            P("mp", "dp"),
            P(None, None, "dp", "mp"),
            P(None, None, "dp", "mp"),
            P(None, None, "dp", "mp"),
            P(None, None, "dp", "mp"),
            P("mp", "dp", None),
            P("mp", "dp", None),
            P("mp", "dp"),
            P("mp", "dp"),
            P(None, None, "dp", "mp"),
            P(None, None, "dp", "mp"),
            P("mp", "dp", None),
            P("mp", "dp"),
        ),
        check_vma=False,
    )
```

profile of v0, /device:TPU:0, one launch (start us, length us, event | category | flops | bytes accessed | tf_op | source)
XLA Modules:
  0.0 581.1 jit_solution(16968905555778703401)
XLA Ops:
  8.3 48.3 %all_gather.26 = bf16[3,3,256,128]{3,2,1,0:T(8,128)(2,1)} all-gather(bf16[3,3,16,128]{3,2,1,0:T(8,128)(2,1)S(1)} %convert_element_type.150), channel_id=1, replica_groups=mesh['dp'=16,'mp'=2] {'dp'}, dimensions={2}, use_global_device_ids=true | all-gather | bytes 626688 | tf_op jit(solution)/shard_map/all_gather | solution.py:123
  57.5 41.0 %all_gather.28 = bf16[3,3,256,128]{3,2,1,0:T(8,128)(2,1)} all-gather(bf16[3,3,16,128]{3,2,1,0:T(8,128)(2,1)S(1)} %convert_element_type.152), channel_id=1, replica_groups=mesh['dp'=16,'mp'=2] {'dp'}, dimensions={2}, use_global_device_ids=true | all-gather | bytes 626688 | tf_op jit(solution)/shard_map/all_gather | solution.py:124
  100.1 38.8 %all-reduce.4 = bf16[256]{0:T(256)(128)(2,1)S(1)} all-reduce(bf16[256]{0:T(256)(128)(2,1)S(1)} %dynamic-update-slice), channel_id=1, replica_groups=mesh['dp'=16,'mp'=2] {'dp'}, use_global_device_ids=true, to_apply=%add.4 | all-reduce | flops 256 | bytes 1024
  138.9 1.8 all-gather
  144.4 37.2 %all_gather.30 = bf16[1,256,601]{2,1,0:T(8,128)(2,1)S(1)} all-gather(bf16[1,16,601]{2,1,0:T(8,128)(2,1)S(1)} %convert_element_type.157), channel_id=1, replica_groups=mesh['dp'=16,'mp'=2] {'dp'}, dimensions={1}, use_global_device_ids=true | all-gather | bytes 326944 | tf_op jit(solution)/shard_map/all_gather | solution.py:125
  183.4 1.4 add_reduce_fusion
  184.8 1.4 add_reduce_fusion.1
  186.2 2.4 all_gather.31
  189.5 2.0 fusion.6
  192.3 2.0 convolution_multiply_fusion.3
  197.4 2.1 fusion.5
  207.8 2.1 fusion.7
  216.4 1.2 fusion
  220.8 1.3 fusion.15
  222.1 1.2 fusion.14
  223.4 1.2 fusion.13
  224.6 1.2 fusion.12
  225.9 1.2 fusion.11
  227.1 1.3 fusion.10
  228.4 1.2 fusion.9
  235.6 2.0 add_multiply_fusion
  238.7 2.0 fusion.8
  247.1 1.7 add_multiply_fusion.1
  251.8 2.5 all-reduce.5
  257.3 1.5 reduce-scatter.10.cloned.1.call-done
  258.8 80.4 %reduce-scatter.22.cloned.1.call-done = f32[16,1]{1,0:T(8,128)} async-done(((f32[256,1]{1,0:T(8,128)}), f32[16,1]{1,0:T(8,128)}) %reduce-scatter.22.cloned.1.call-update) | async-done | bytes 80
  340.5 75.6 %reduce-scatter.20.cloned.1.call-done = f32[1,16,601]{2,1,0:T(8,128)} async-done(((f32[1,256,601]{2,1,0:T(8,128)}), f32[1,16,601]{2,1,0:T(8,128)}) %reduce-scatter.20.cloned.1.call-update) | async-done | bytes 38480 | tf_op jit(solution)/shard_map/reduce_scatter | solution.py:219
  416.1 1.4 divide_subtract_fusion.2
  417.6 77.1 %reduce-scatter.16.cloned.1.call-done = f32[3,3,16,128]{3,2,1,0:T(8,128)} async-done(((f32[3,3,256,128]{3,2,1,0:T(8,128)}), f32[3,3,16,128]{3,2,1,0:T(8,128)}) %reduce-scatter.16.cloned.1.call-update) | async-done | bytes 73744 | tf_op jit(solution)/shard_map/reduce_scatter | solution.py:218
  494.6 1.6 divide_subtract_fusion
  496.2 76.8 %reduce-scatter.12.cloned.1.call-done = f32[3,3,16,128]{3,2,1,0:T(8,128)} async-done(((f32[3,3,256,128]{3,2,1,0:T(8,128)}), f32[3,3,16,128]{3,2,1,0:T(8,128)}) %reduce-scatter.12.cloned.1.call-update) | async-done | bytes 73744 | tf_op jit(solution)/shard_map/reduce_scatter | solution.py:217
  573.0 1.6 divide_subtract_fusion.1
  (238 shorter events, 46.9 us)
Async XLA Ops:
  7.2 136.1 %copy-start = (bf16[2,19,19,256]{3,0,2,1:T(2,128)(2,1)S(1)}, bf16[2,19,19,256]{3,0,2,1:T(2,128)(2,1)}, u32[]{:S(2)}) copy-start(bf16[2,19,19,256]{3,0,2,1:T(2,128)(2,1)} %param.16) | copy-start | bytes 1108996
  7.2 91.4 %copy-start.38 = (u32[32]{0:T(128)S(1)}, u32[32]{0:T(128)}, u32[]{:S(2)}) copy-start(u32[32]{0:T(128)} %constant.145) | copy-start | bytes 388
  7.2 91.4 %copy-start.28 = (f32[1,16]{1,0:T(1,128)S(1)}, f32[1,16]{1,0:T(1,128)}, u32[]{:S(2)}) copy-start(f32[1,16]{1,0:T(1,128)} %param.23) | copy-start | bytes 196
  7.2 133.5 %copy-start.36 = (s32[2,2]{1,0:T(2,128)S(1)}, s32[2,2]{1,0:T(2,128)}, u32[]{:S(2)}) copy-start(s32[2,2]{1,0:T(2,128)} %param.17) | copy-start | bytes 52
  7.2 137.1 %copy-start.17 = (f32[1,16,601]{2,1,0:T(8,128)S(1)}, f32[1,16,601]{2,1,0:T(8,128)}, u32[]{:S(2)}) copy-start(f32[1,16,601]{2,1,0:T(8,128)} %param.22) | copy-start | bytes 115396
  7.2 174.4 %copy-start.32 = (s32[2,2]{1,0:T(2,128)S(1)}, s32[2,2]{1,0:T(2,128)}, u32[]{:S(2)}) copy-start(s32[2,2]{1,0:T(2,128)} %param.18) | copy-start | bytes 52
  7.3 174.4 %copy-start.31 = (s32[2,2]{1,0:T(2,128)S(1)}, s32[2,2]{1,0:T(2,128)}, u32[]{:S(2)}) copy-start(s32[2,2]{1,0:T(2,128)} %param.19) | copy-start | bytes 52
  7.3 182.2 %all-gather.4.cloned.1.call-start = ((), (), s32[]{:S(2)}) async-start(), calls=%async_computation.7 | async-start | bytes 1769472 | tf_op jit(solution)/shard_map/all_gather | solution.py:129
  56.6 135.1 %all-gather.6.cloned.1.call-start = ((), (), s32[]{:S(2)}) async-start(), calls=%async_computation.8 | async-start | bytes 1769472 | tf_op jit(solution)/shard_map/all_gather | solution.py:130
  98.5 157.2 %reduce-scatter.18.cloned.1.call-start = ((), (), s32[]{:S(2)}) async-start(), calls=%async_computation.13 | async-start | bytes 1966080 | tf_op jit(solution)/shard_map/reduce_scatter | solution.py:213
  181.6 7.9 %copy-start.26 = (pred[8,3]{0,1:T(4,128)(4,1)S(1)}, pred[8,3]{0,1:T(4,128)(4,1)}, u32[]{:S(2)}) copy-start(pred[8,3]{0,1:T(4,128)(4,1)} %constant.135) | copy-start | bytes 76
  204.5 3.3 copy-start.12
  217.7 38.8 %reduce-scatter.14.cloned.1.call-start = ((), (), s32[]{:S(2)}) async-start(), calls=%async_computation.11 | async-start | bytes 3538944 | tf_op jit(solution)/shard_map/reduce_scatter | solution.py:212
  237.6 3.1 copy-start.6
  237.6 3.8 copy-start.15
  237.6 21.2 %reduce-scatter.10.cloned.1.call-start = ((), (), s32[]{:S(2)}) async-start(), calls=%async_computation.9 | async-start | bytes 3538944 | tf_op jit(solution)/shard_map/reduce_scatter | solution.py:211
  248.9 90.3 %reduce-scatter.22.cloned.1.call-start = ((), (), s32[]{:S(2)}) async-start(), calls=%async_computation.15 | async-start | bytes 139264
  251.5 88.5 %copy-start.29 = (f32[1,16]{1,0:T(1,128)S(1)}, f32[1,16]{1,0:T(1,128)}, u32[]{:S(2)}) copy-start(f32[1,16]{1,0:T(1,128)} %param.30) | copy-start | bytes 196
  251.5 88.5 %copy-start.30 = (f32[1,16]{1,0:T(1,128)S(1)}, f32[1,16]{1,0:T(1,128)}, u32[]{:S(2)}) copy-start(f32[1,16]{1,0:T(1,128)} %param.31) | copy-start | bytes 196
  251.5 164.7 %copy-start.18 = (f32[1,16,601]{2,1,0:T(8,128)S(1)}, f32[1,16,601]{2,1,0:T(8,128)}, u32[]{:S(2)}) copy-start(f32[1,16,601]{2,1,0:T(8,128)} %param.22) | copy-start | bytes 115396
  251.5 164.6 %copy-start.24 = (f32[1,16,601]{2,1,0:T(8,128)S(1)}, f32[1,16,601]{2,1,0:T(8,128)}, u32[]{:S(2)}) copy-start(f32[1,16,601]{2,1,0:T(8,128)} %param.28) | copy-start | bytes 115396
  251.5 164.6 %copy-start.25 = (f32[1,16,601]{2,1,0:T(8,128)S(1)}, f32[1,16,601]{2,1,0:T(8,128)}, u32[]{:S(2)}) copy-start(f32[1,16,601]{2,1,0:T(8,128)} %param.29) | copy-start | bytes 115396
  251.5 243.1 %copy-start.13 = (f32[3,3,16,128]{3,2,1,0:T(8,128)S(1)}, f32[3,3,16,128]{3,2,1,0:T(8,128)}, u32[]{:S(2)}) copy-start(f32[3,3,16,128]{3,2,1,0:T(8,128)} %param.21) | copy-start | bytes 221188
  251.5 243.1 %copy-start.20 = (f32[3,3,16,128]{3,2,1,0:T(8,128)S(1)}, f32[3,3,16,128]{3,2,1,0:T(8,128)}, u32[]{:S(2)}) copy-start(f32[3,3,16,128]{3,2,1,0:T(8,128)} %param.26) | copy-start | bytes 221188
  251.5 243.1 %copy-start.21 = (f32[3,3,16,128]{3,2,1,0:T(8,128)S(1)}, f32[3,3,16,128]{3,2,1,0:T(8,128)}, u32[]{:S(2)}) copy-start(f32[3,3,16,128]{3,2,1,0:T(8,128)} %param.27) | copy-start | bytes 221188
  251.5 321.5 %copy-start.14 = (f32[3,3,16,128]{3,2,1,0:T(8,128)S(1)}, f32[3,3,16,128]{3,2,1,0:T(8,128)}, u32[]{:S(2)}) copy-start(f32[3,3,16,128]{3,2,1,0:T(8,128)} %param.20) | copy-start | bytes 221188
  251.6 321.5 %copy-start.22 = (f32[3,3,16,128]{3,2,1,0:T(8,128)S(1)}, f32[3,3,16,128]{3,2,1,0:T(8,128)}, u32[]{:S(2)}) copy-start(f32[3,3,16,128]{3,2,1,0:T(8,128)} %param.24) | copy-start | bytes 221188
  251.6 321.4 %copy-start.23 = (f32[3,3,16,128]{3,2,1,0:T(8,128)S(1)}, f32[3,3,16,128]{3,2,1,0:T(8,128)}, u32[]{:S(2)}) copy-start(f32[3,3,16,128]{3,2,1,0:T(8,128)} %param.25) | copy-start | bytes 221188
  255.7 160.4 %reduce-scatter.20.cloned.1.call-start = ((), (), s32[]{:S(2)}) async-start(), calls=%async_computation.14 | async-start | bytes 696320 | tf_op jit(solution)/shard_map/reduce_scatter | solution.py:219
  256.5 238.2 %reduce-scatter.16.cloned.1.call-start = ((), (), s32[]{:S(2)}) async-start(), calls=%async_computation.12 | async-start | bytes 1253376 | tf_op jit(solution)/shard_map/reduce_scatter | solution.py:218
  257.2 315.8 %reduce-scatter.12.cloned.1.call-start = ((), (), s32[]{:S(2)}) async-start(), calls=%async_computation.10 | async-start | bytes 1253376 | tf_op jit(solution)/shard_map/reduce_scatter | solution.py:217
  340.0 234.7 %copy-start.27 = (f32[1,16]{1,0:T(1,128)}, f32[1,16]{1,0:T(1,128)S(1)}, u32[]{:S(2)}) copy-start(f32[1,16]{1,0:T(1,128)S(1)} %copy.107) | copy-start | bytes 196
  (16 other events, 23.1 us)
Sparse Core Ops, SparseCore 0:
  56.7 4.7 all-gather.3
  98.7 6.9 all-gather.5
  217.8 6.4 reduce-scatter.17
  237.7 7.6 reduce-scatter.13
  249.0 9.7 reduce-scatter.9
  260.9 78.2 reduce-scatter.21
  342.0 74.0 reduce-scatter.19
  419.0 75.6 reduce-scatter.15
  497.5 75.4 reduce-scatter.11
where the time goes:
time: 582 us; the launch traced here: 581 us
  waiting for transfers between devices  313 us (54%)
  blocking collectives  172 us (30%)
  matrix products  33.7 us (6%)
  other arithmetic  24.3 us (4%)
  between operations  19.6 us (3%)
  local copies, waits for them, and re-layouts  18.2 us (3%)
    unnamed x10, waiting for transfers between devices  81.8 us
    reduce_scatter x1, waiting for transfers between devices, local(): lax.psum_scatter(second_grad, 'dp', scatter_dimension=2, tiled=True)  77.1 us
    reduce_scatter x1, waiting for transfers between devices, local(): lax.psum_scatter(first_grad, 'dp', scatter_dimension=2, tiled=True)  76.8 us
    reduce_scatter x1, waiting for transfers between devices, local(): lax.psum_scatter(head_grad, 'dp', scatter_dimension=1, tiled=True)  75.6 us
    all_gather x1, blocking collectives, local(): lax.all_gather(kernel_first.astype(jnp.bfloat16), 'dp', axis=2, tiled=True)  48.3 us
    unnamed x2, blocking collectives  41.3 us
    all_gather x1, blocking collectives, local(): lax.all_gather(kernel_second.astype(jnp.bfloat16), 'dp', axis=2, tiled=True)  41 us
    all_gather x1, blocking collectives, local(): lax.all_gather(head_weight.astype(jnp.bfloat16), 'dp', axis=1, tiled=True)  37.2 us
  transfers between devices with their start and end apart: 9, of which 5 were waited for; matrix products, arithmetic and copies ran while one was open for 8% of the time, Pallas kernels for 0%

commit v1 on v0

v1 whole, which is shorter than its diff:
```python
import functools

import jax
import jax.numpy as jnp
from jax import lax
from jax.experimental import pallas as pl
from jax.experimental.pallas import tpu as pltpu
from jax.sharding import PartitionSpec as P

CHANNELS = 256
LANES = 128
TILE = 16


head_scale = 4.0
soft_cap = 15.0
eps_norm = 1e-05
beta_one = 0.9
beta_two = 0.999
step_size = 0.1
eps_adam = 1e-08


def adam_update(param, grad, mean, square):
    mean_new = beta_one * mean + (1.0 - beta_one) * grad
    square_new = beta_two * square + (1.0 - beta_two) * grad * grad
    param_new = param - step_size * mean_new / (jnp.sqrt(square_new) + eps_adam)
    return (param_new, mean_new, square_new)


def round_up(value, step):
    return -(-value // step) * step


def spread(block, axis):
    copies = jnp.broadcast_to(block[None], (lax.axis_size(axis),) + block.shape)
    return lax.all_to_all(copies, axis, 0, 0)


def row_pad(block, axis):
    short = -block.shape[axis] % TILE
    if not short:
        return block
    widths = [(0, 0)] * block.ndim
    widths[axis] = (0, short)
    return jnp.pad(block, widths)


def gather_weights(kernel_first, kernel_second, head_weight, action_embed):
    rows = kernel_first.shape[2]
    buckets = head_weight.shape[2]
    blocks = round_up(buckets, LANES) // LANES
    head = jnp.pad(head_weight[0], ((0, 0), (0, blocks * LANES - buckets)))
    head = head.reshape(rows, blocks, LANES).transpose(1, 0, 2)
    embed = jnp.pad(action_embed, ((0, TILE - 1), (0, LANES - rows)))
    packed = jnp.concatenate(
        [
            row_pad(kernel_first.astype(jnp.bfloat16).reshape(-1, LANES), 0),
            row_pad(kernel_second.astype(jnp.bfloat16).reshape(-1, LANES), 0),
            row_pad(head.astype(jnp.bfloat16).reshape(-1, LANES), 0),
            embed.astype(jnp.bfloat16),
        ]
    )
    everything = spread(spread(packed, "dp"), "mp")
    embed_used = everything[:, :, -TILE, :rows].reshape(everything.shape[0], CHANNELS)
    if rows != TILE:
        everything = regroup(everything, rows, blocks)
    return (everything, embed_used.astype(jnp.float32))


def regroup(everything, rows, blocks):
    cores, shards = everything.shape[:2]
    groups = CHANNELS // TILE
    parts = []
    begin = 0
    for taps in (9, 9, blocks):
        part = everything[:, :, begin : begin + taps * rows]
        begin += round_up(taps * rows, TILE)
        part = part.reshape(cores, groups, shards // groups, taps, rows, LANES)
        parts.append(part.transpose(0, 1, 3, 2, 4, 5).reshape(cores, groups, taps * TILE, LANES))
    parts.append(jnp.zeros((cores, groups, TILE, LANES), everything.dtype))
    return jnp.concatenate(parts, axis=2)


def ungroup(packed, rows, blocks, shards):
    cores, groups = packed.shape[:2]
    parts = []
    begin = 0
    for taps in (9, 9, blocks):
        part = packed[:, :, begin : begin + taps * TILE]
        begin += taps * TILE
        part = part.reshape(cores, groups, taps, shards // groups, rows, LANES)
        part = part.transpose(0, 1, 3, 2, 4, 5).reshape(cores, shards, taps * rows, LANES)
        parts.append(row_pad(part, 2))
    parts.append(jnp.repeat(packed[:, :, begin:], shards // groups, axis=1))
    return jnp.concatenate(parts, axis=2)


def scatter_grads(packed, rows, buckets):
    blocks = round_up(buckets, LANES) // LANES
    shards = lax.axis_size("dp")
    if rows != TILE:
        packed = ungroup(packed, rows, blocks, shards)
    halves = lax.all_to_all(packed, "mp", 0, 0)
    summed = jnp.sum(halves.astype(jnp.float32), axis=0).astype(jnp.bfloat16)
    owned = lax.all_to_all(summed, "dp", 0, 0)
    total = jnp.sum(owned.astype(jnp.float32), axis=0)
    step = round_up(9 * rows, TILE)
    first = total[: 9 * rows].reshape(3, 3, rows, LANES)
    second = total[step : step + 9 * rows].reshape(3, 3, rows, LANES)
    head = total[2 * step : 2 * step + blocks * rows].reshape(blocks, rows, LANES)
    head = head.transpose(1, 0, 2).reshape(1, rows, blocks * LANES)[:, :, :buckets]
    embed = total[-TILE : CHANNELS // LANES - TILE].reshape(1, CHANNELS)
    embed = lax.dynamic_slice_in_dim(embed, lax.axis_index("dp") * rows, rows, 1)
    return (first, second, head, embed)


def nn(left, right):
    return jnp.dot(left, right, preferred_element_type=jnp.float32)


def nt(left, right):
    return lax.dot_general(left, right, (((1,), (1,)), ((), ())), preferred_element_type=jnp.float32)


def tn(left, right):
    return lax.dot_general(left, right, (((0,), (0,)), ((), ())), preferred_element_type=jnp.float32)


def window_kernel(
    spots,
    passes,
    values,
    rewards,
    every,
    states,
    mask,
    embed,
    out,
    first,
    second,
    head,
    padded,
    fields,
    hiddens,
    taps,
    pres,
    sums,
    inners,
    branches,
    *,
    count,
    unroll,
    board,
    width,
    extent,
    buckets,
    blocks,
    total,
):
    cells = board * board
    base = 8
    scale = (9.0 * CHANNELS) ** (-0.5)
    cores = CHANNELS // LANES
    groups = CHANNELS // TILE
    spread_cols = blocks * LANES
    for core in range(cores):
        lanes = slice(core * LANES, (core + 1) * LANES)
        for group in range(groups):
            rows = slice(group * TILE, (group + 1) * TILE)
            for tap in range(9):
                at = tap * CHANNELS + group * TILE
                first[at : at + TILE, lanes] = every[core, group, tap * TILE : (tap + 1) * TILE, :]
                two = (9 + tap) * TILE
                second[at : at + TILE, lanes] = every[core, group, two : two + TILE, :]
    for which in range(2):
        for group in range(groups):
            for block in range(blocks):
                at = (18 + block) * TILE
                head[
                    which, group * TILE : (group + 1) * TILE, block * LANES : (block + 1) * LANES
                ] = every[which, group, at : at + TILE, :]
    padded[...] = jnp.zeros(padded.shape, jnp.float32)
    inside = jnp.broadcast_to(mask[...], (extent, CHANNELS)) > 0.5
    cell_at = lax.broadcasted_iota(jnp.int32, (extent, CHANNELS), 0)
    lane_at = lax.broadcasted_iota(jnp.int32, (8, spread_cols), 1)
    row_at = lax.broadcasted_iota(jnp.int32, (TILE, 1), 0)

    def lay_out(field, target, begin, flip):
        padded[base + width : base + width + extent, :] = field
        for tap in range(9):
            start = base + (tap // 3) * width + tap % 3 - 1
            slot = 8 - tap if flip else tap
            target[begin : begin + extent, slot * CHANNELS : (slot + 1) * CHANNELS] = padded[
                start : start + extent, :
            ].astype(jnp.bfloat16)

    def taps_nt(source, begin, kernel):
        result = None
        for tap in range(9):
            cols = slice(tap * CHANNELS, (tap + 1) * CHANNELS)
            part = nt(source[begin : begin + extent, cols], kernel[cols, :])
            result = part if result is None else result + part
        return result

    def grand(block):
        return jnp.sum(jnp.sum(block, axis=0, keepdims=True), axis=1, keepdims=True)

    pooled_rows = jnp.zeros((TILE, CHANNELS), jnp.float32)
    grad_rows = [jnp.zeros((TILE, spread_cols), jnp.float32) for _ in range(2)]
    factors = {}
    pulls = {}
    for n in range(count):
        state = states[n].astype(jnp.float32)
        for k in range(unroll):
            slot = k * count + n
            begin = slot * extent
            plane = cell_at == spots[n, k]
            extra = jnp.where(inside, passes[n, k].astype(jnp.float32) * embed[1:2, :], 0.0)
            mixed = state + jnp.where(plane, embed[0:1, :], 0.0) + extra
            lay_out(mixed, fields, begin, False)
            pre = scale * nn(fields[begin : begin + extent, :], first[...])
            pres[slot] = pre
            hidden = jnp.where(inside, pre * jax.nn.sigmoid(pre), 0.0)
            lay_out(hidden, hiddens, begin, False)
            branch = taps_nt(hiddens, begin, second)
            summed = jnp.where(inside, mixed + scale * branch, 0.0)
            sums[slot] = summed
            factor = lax.rsqrt(grand(summed * summed) / (cells * CHANNELS) + eps_norm)
            factors[slot] = factor
            state = summed * factor
            pooled = (jnp.sum(state, axis=0, keepdims=True) / cells).astype(jnp.bfloat16)
            pooled_rows = jnp.where(row_at == slot, pooled.astype(jnp.float32), pooled_rows)
            eight = jnp.broadcast_to(pooled.astype(jnp.float32), (8, CHANNELS)).astype(jnp.bfloat16)
            pull = jnp.zeros((8, CHANNELS), jnp.float32)
            for which, targets in enumerate((values, rewards)):
                raw = head_scale * nn(eight, head[which])
                squashed = jnp.tanh(raw / soft_cap)
                raised = jnp.where(lane_at < buckets, jnp.exp(soft_cap * squashed), 0.0)
                chances = raised / jnp.sum(raised, axis=1, keepdims=True)
                picked = jnp.where(lane_at == targets[n, k], 1.0, 0.0)
                logit_grad = (chances - picked) * (1.0 - squashed * squashed) / total
                rounded = logit_grad.astype(jnp.bfloat16)
                grad_rows[which] = jnp.where(
                    row_at == slot, rounded.astype(jnp.float32)[0:1, :], grad_rows[which]
                )
                pull = pull + nt(rounded, head[which])
            pulls[slot] = head_scale * pull[0:1, :]
    embed_grads = [jnp.zeros((1, CHANNELS), jnp.float32) for _ in range(2)]
    for n in range(count):
        carry = jnp.zeros((extent, CHANNELS), jnp.float32)
        for k in range(unroll - 1, -1, -1):
            slot = k * count + n
            begin = slot * extent
            factor = factors[slot]
            summed = sums[slot]
            state_grad = carry + jnp.where(inside, pulls[slot] / cells, 0.0)
            shared = grand(state_grad * summed) / (cells * CHANNELS)
            summed_grad = factor * state_grad - factor * factor * factor * summed * shared
            branches[begin : begin + extent, :] = summed_grad.astype(jnp.bfloat16)
            lay_out(summed_grad, taps, 0, True)
            hidden_grad = scale * nn(taps[...], second[...])
            pre = pres[slot]
            sig = jax.nn.sigmoid(pre)
            inner = jnp.where(inside, hidden_grad * (sig * (1.0 + pre * (1.0 - sig))), 0.0)
            inners[begin : begin + extent, :] = inner.astype(jnp.bfloat16)
            lay_out(inner, taps, 0, True)
            carry = jnp.where(inside, summed_grad + scale * taps_nt(taps, 0, first), 0.0)
            embed_grads[0] = embed_grads[0] + jnp.sum(
                jnp.where(cell_at == spots[n, k], carry, 0.0), axis=0, keepdims=True
            )
            embed_grads[1] = embed_grads[1] + passes[n, k].astype(jnp.float32) * jnp.sum(
                carry, axis=0, keepdims=True
            )
    turned_inner = inners[...].T
    turned_branch = branches[...].T
    for tap in range(9):
        cols = slice(tap * CHANNELS, (tap + 1) * CHANNELS)
        one = (scale * nn(turned_inner, fields[:, cols])).T.astype(jnp.bfloat16)
        two = (scale * nn(turned_branch, hiddens[:, cols])).astype(jnp.bfloat16)
        for core in range(cores):
            lanes = slice(core * LANES, (core + 1) * LANES)
            for group in range(groups):
                rows = slice(group * TILE, (group + 1) * TILE)
                out[core, group, tap * TILE : (tap + 1) * TILE, :] = one[rows, lanes]
                out[core, group, (9 + tap) * TILE : (10 + tap) * TILE, :] = two[rows, lanes]
    pooled_bf = pooled_rows.astype(jnp.bfloat16)
    for which in range(2):
        grown = head_scale * tn(pooled_bf, grad_rows[which].astype(jnp.bfloat16))
        grown = grown.astype(jnp.bfloat16)
        line = jnp.where(
            row_at == 0,
            embed_grads[which][:, :LANES],
            jnp.where(row_at == 1, embed_grads[which][:, LANES:], 0.0),
        ).astype(jnp.bfloat16)
        for group in range(groups):
            rows = slice(group * TILE, (group + 1) * TILE)
            for block in range(blocks):
                at = (18 + block) * TILE
                out[which, group, at : at + TILE, :] = grown[
                    rows, block * LANES : (block + 1) * LANES
                ]
            at = (18 + blocks) * TILE
            out[which, group, at : at + TILE, :] = line


def window(every, embed, states, moves, values, rewards, buckets, total):
    count, board = states.shape[:2]
    unroll = moves.shape[1]
    cells = board * board
    width = round_up(board + 1, 8)
    extent = round_up(board * width, TILE)
    blocks = round_up(buckets, LANES) // LANES
    states = jnp.pad(states, ((0, 0), (0, 0), (0, width - board), (0, 0)))
    states = states.reshape(count, board * width, CHANNELS)
    states = jnp.pad(states, ((0, 0), (0, extent - board * width), (0, 0)))
    passes = (moves == cells).astype(jnp.int32)
    spots = jnp.where(moves == cells, -1, moves // board * width + moves % board)
    at = jnp.arange(extent)
    mask = ((at % width < board) & (at // width < board)).astype(jnp.float32)[:, None]
    deep = count * unroll * extent
    body = functools.partial(
        window_kernel,
        count=count,
        unroll=unroll,
        board=board,
        width=width,
        extent=extent,
        buckets=buckets,
        blocks=blocks,
        total=total,
    )
    smem = pl.BlockSpec(memory_space=pltpu.SMEM)
    vmem = pl.BlockSpec(memory_space=pltpu.VMEM)
    return pl.pallas_call(
        body,
        out_shape=jax.ShapeDtypeStruct(every.shape, jnp.bfloat16),
        in_specs=[smem] * 4 + [vmem] * 4,
        out_specs=vmem,
        scratch_shapes=[
            pltpu.VMEM((9 * CHANNELS, CHANNELS), jnp.bfloat16),
            pltpu.VMEM((9 * CHANNELS, CHANNELS), jnp.bfloat16),
            pltpu.VMEM((2, CHANNELS, blocks * LANES), jnp.bfloat16),
            pltpu.VMEM((extent + 2 * width + 16, CHANNELS), jnp.float32),
            pltpu.VMEM((deep, 9 * CHANNELS), jnp.bfloat16),
            pltpu.VMEM((deep, 9 * CHANNELS), jnp.bfloat16),
            pltpu.VMEM((extent, 9 * CHANNELS), jnp.bfloat16),
            pltpu.VMEM((count * unroll, extent, CHANNELS), jnp.float32),
            pltpu.VMEM((count * unroll, extent, CHANNELS), jnp.float32),
            pltpu.VMEM((deep, CHANNELS), jnp.bfloat16),
            pltpu.VMEM((deep, CHANNELS), jnp.bfloat16),
        ],
        compiler_params=pltpu.CompilerParams(vmem_limit_bytes=56 * 1024 * 1024),
    )(spots, passes, values, rewards, every, states, mask, embed)


def local(
    hidden_state,
    actions,
    value_target,
    reward_target,
    kernel_first,
    kernel_second,
    head_weight,
    action_embed,
    first_mean,
    first_square,
    second_mean,
    second_square,
    head_mean,
    head_square,
    embed_mean,
    embed_square,
):
    total = hidden_state.shape[0] * lax.axis_size("dp")
    rows = kernel_first.shape[2]
    buckets = head_weight.shape[2]
    every, embed = gather_weights(kernel_first, kernel_second, head_weight, action_embed)
    count = hidden_state.shape[0] // lax.axis_size("mp")
    begin = lax.axis_index("mp") * count
    states = lax.dynamic_slice_in_dim(hidden_state, begin, count, 0)
    moves = lax.dynamic_slice_in_dim(actions, begin, count, 0)
    values = lax.dynamic_slice_in_dim(value_target, begin, count, 0)
    rewards = lax.dynamic_slice_in_dim(reward_target, begin, count, 0)
    packed = window(every, embed, states, moves, values, rewards, buckets, total)
    first_grad, second_grad, head_grad, embed_grad = scatter_grads(packed, rows, buckets)
    first_new, first_mean_new, first_square_new = adam_update(
        kernel_first, first_grad, first_mean, first_square
    )
    second_new, second_mean_new, second_square_new = adam_update(
        kernel_second, second_grad, second_mean, second_square
    )
    head_new, head_mean_new, head_square_new = adam_update(
        head_weight, head_grad, head_mean, head_square
    )
    embed_new, embed_mean_new, embed_square_new = adam_update(
        action_embed, embed_grad, embed_mean, embed_square
    )
    return (
        first_new,
        second_new,
        head_new,
        embed_new,
        first_mean_new,
        first_square_new,
        second_mean_new,
        second_square_new,
        head_mean_new,
        head_square_new,
        embed_mean_new,
        embed_square_new,
        first_grad,
        second_grad,
        head_grad,
        embed_grad,
    )


def solution(mesh):
    placed = (
        P("dp", None, None, None),
        P("dp", None),
        P("dp", None),
        P("dp", None),
        P(None, None, "dp", "mp"),
        P(None, None, "dp", "mp"),
        P("mp", "dp", None),
        P("mp", "dp"),
        P(None, None, "dp", "mp"),
        P(None, None, "dp", "mp"),
        P(None, None, "dp", "mp"),
        P(None, None, "dp", "mp"),
        P("mp", "dp", None),
        P("mp", "dp", None),
        P("mp", "dp"),
        P("mp", "dp"),
    )
    return jax.shard_map(
        local,
        mesh=mesh,
        in_specs=placed,
        out_specs=(
            P(None, None, "dp", "mp"),
            P(None, None, "dp", "mp"),
            P("mp", "dp", None),
            P("mp", "dp"),
            P(None, None, "dp", "mp"),
            P(None, None, "dp", "mp"),
            P(None, None, "dp", "mp"),
            P(None, None, "dp", "mp"),
            P("mp", "dp", None),
            P("mp", "dp", None),
            P("mp", "dp"),
            P("mp", "dp"),
            P(None, None, "dp", "mp"),
            P(None, None, "dp", "mp"),
            P("mp", "dp", None),
            P("mp", "dp"),
        ),
        check_vma=False,
    )
```

time: 582 us -> 132 us (0.23)
  waiting for transfers between devices: 313 us -> 64.7 us
  blocking collectives: 172 us -> 13.8 us
  matrix products: 33.7 us -> 0 us
  between operations: 19.6 us -> 0.93 us
  Pallas kernels: 0 us -> 17.7 us
  starting transfers between devices: 0.59 us -> 16.2 us
  other arithmetic: 24.3 us -> 10.3 us
  local copies, waits for them, and re-layouts: 18.2 us -> 5.68 us
    reduce_scatter x6 -> x0, waiting for transfers between devices: 231 us -> none  [the longest x1 77.1 us: local(): lax.psum_scatter(second_grad, 'dp', scatter_dimension=2, tiled=True)]
    all_gather x5 -> x0, blocking collectives: 131 us -> none  [the longest x1 48.3 us: local(): lax.all_gather(kernel_first.astype(jnp.bfloat16), 'dp', axis=2, tiled=True)]
    unnamed x10 -> x0, waiting for transfers between devices: 81.8 us -> none
    all_to_all x0 -> x2, waiting for transfers between devices: none -> 64.7 us  [the longest x1 34.2 us: scatter_grads(): owned = lax.all_to_all(summed, 'dp', 0, 0)]
    unnamed x2 -> x0, blocking collectives: 41.3 us -> none
    dot_general x44 -> x0, matrix products: 21.2 us -> none  [the longest x18 14.7 us: tap_products(): lax.dot_general(flat_grad, window, (((0,), (0,)), ((), ())), preferred_el...]
    pallas_call x0 -> x1, Pallas kernels: none -> 17.7 us  [window(): pl.pallas_call(body, out_shape=jax.ShapeDtypeStruct(every.shape, jnp.bflo...]
    all_to_all x0 -> x2, starting transfers between devices: none -> 16.2 us  [the longest x1 8.34 us: spread(): return lax.all_to_all(copies, axis, 0, 0)]
  transfers between devices with their start and end apart: 9 -> 2, of which waited for: 5 -> 2; matrix products, arithmetic and copies ran while one was open for 8% -> 3% of each run, Pallas kernels for 0% -> 0%
where the time goes in v1:
time: 132 us; the launch traced here: 129 us
  waiting for transfers between devices  64.7 us (49%)
  Pallas kernels  17.7 us (13%)
  starting transfers between devices  16.2 us (12%)
  blocking collectives  13.8 us (10%)
  other arithmetic  10.3 us (8%)
  local copies, waits for them, and re-layouts  5.68 us (4%)
    all_to_all x1, waiting for transfers between devices, scatter_grads(): owned = lax.all_to_all(summed, 'dp', 0, 0)  34.2 us
    all_to_all x1, waiting for transfers between devices, spread(): return lax.all_to_all(copies, axis, 0, 0)  30.5 us
    pallas_call x1, Pallas kernels, window(): pl.pallas_call(body, out_shape=jax.ShapeDtypeStruct(every.shape, jnp.bflo...  17.7 us
    all_to_all x1, starting transfers between devices, spread(): return lax.all_to_all(copies, axis, 0, 0)  8.34 us
    all_to_all x1, starting transfers between devices, scatter_grads(): owned = lax.all_to_all(summed, 'dp', 0, 0)  7.89 us
    all_to_all x1, blocking collectives, scatter_grads(): halves = lax.all_to_all(packed, 'mp', 0, 0)  7.55 us
    all_to_all x1, blocking collectives, spread(): return lax.all_to_all(copies, axis, 0, 0)  6.26 us
    sub x4, other arithmetic, adam_update(): param_new = param - step_size * mean_new / (jnp.sqrt(square_new) + eps_adam)  2.7 us
  transfers between devices with their start and end apart: 2, of which 2 were waited for; matrix products, arithmetic and copies ran while one was open for 3% of the time, Pallas kernels for 0%

profile of v1, /device:TPU:0, one launch (start us, length us, event | category | flops | bytes accessed | tf_op | source)
XLA Modules:
  0.0 129.5 jit_solution(16897115237093523447)
XLA Ops:
  0.6 0.0 copy-start
  0.7 0.8 convert_bitcast_fusion
  1.6 0.9 convert_element_type.46
  2.5 0.9 convert_element_type.47
  3.4 0.7 convert.12
  4.0 0.0 copy-start.17
  4.1 1.5 %broadcast_in_dim.8 = bf16[16,384,128]{2,1,0:T(8,128)(2,1)} broadcast(bf16[384,128]{1,0:T(8,128)(2,1)S(1)} %fusion.12), dimensions={1,2} | broadcast | bytes 1671168 | tf_op jit(solution)/shard_map/broadcast_in_dim | solution.py:36
  5.5 8.3 %all-to-all-start = ((bf16[16,384,128]{2,1,0:T(8,128)(2,1)}), bf16[16,384,128]{2,1,0:T(8,128)(2,1)S(1)}, u32[]{:S(2)}, u32[]{:S(2)}) async-start(bf16[16,384,128]{2,1,0:T(8,128)(2,1)} %broadcast_in_dim.8), calls=%async_computation | async-start | bytes 3145728 | tf_op jit(solution)/shard_map/all_to_all | solution.py:37
  13.9 0.4 constant_dynamic-slice_fusion.1
  14.4 0.7 pad.21.states
  15.1 0.5 compare_convert_fusion.passes
  15.6 0.5 compare_select_fusion.spots
  16.1 0.5 constant_dynamic-slice_fusion.2
  16.7 0.8 fusion.10.mask
  17.5 30.5 %all-to-all-done = bf16[16,384,128]{2,1,0:T(8,128)(2,1)S(1)} async-done(((bf16[16,384,128]{2,1,0:T(8,128)(2,1)}), bf16[16,384,128]{2,1,0:T(8,128)(2,1)S(1)}, u32[]{:S(2)}, u32[]{:S(2)}) %all-to-all-start) | async-done | bytes 1572896 | tf_op jit(solution)/shard_map/all_to_all | solution.py:37
  48.0 0.7 broadcast_in_dim.10
  48.7 6.3 %all_to_all.20.every = bf16[2,16,384,128]{3,2,1,0:T(8,128)(2,1)S(1)} all-to-all(bf16[2,16,384,128]{3,2,1,0:T(8,128)(2,1)S(1)} %broadcast_in_dim.10), channel_id=1, replica_groups=mesh['dp'=16,'mp'=2] {'mp'}, dimensions={0} | all-to-all | bytes 6291456 | tf_op jit(solution)/shard_map/all_to_all | solution.py:37
  55.0 0.1 fusion.16
  55.0 0.8 reshape.132.embed
  55.8 0.8 copy-done.1
  56.6 17.7 %shard_map.279 = bf16[2,16,384,128]{3,2,1,0:T(8,128)(2,1)} custom-call(s32[1,2]{1,0:T(1,128)} %compare_select_fusion.spots, s32[1,2]{1,0:T(1,128)} %compare_convert_fusion.passes, s32[1,2]{1,0:T(1,128)} %get-tuple-element.33.values, s32[1,2]{1,0:T(1,128)} %get-tuple-element.32.rewards, bf16[2,16,384,128]{3,2,1,0:T(8,128)(2,1)} %copy-done.1, ...), custom_call_target="tpu_custom_call" | custom-call | tf_op jit(solution)/shard_map/pallas_call | solution.py:335
  74.3 7.5 %all_to_all.21 = bf16[2,16,384,128]{3,2,1,0:T(8,128)(2,1)S(1)} all-to-all(bf16[2,16,384,128]{3,2,1,0:T(8,128)(2,1)} %shard_map.279), channel_id=1, replica_groups=mesh['dp'=16,'mp'=2] {'mp'}, dimensions={0} | all-to-all | bytes 6291456 | tf_op jit(solution)/shard_map/all_to_all | solution.py:104
  81.9 2.2 %reduce_sum.21 = bf16[16,384,128]{2,1,0:T(8,128)(2,1)} reduce(bf16[2,16,384,128]{3,2,1,0:T(8,128)(2,1)S(1)} %all_to_all.21, bf16[]{:T(256)} %constant.41.clone.1), dimensions={0}, to_apply=%region_0.1 | reduce | flops 786432 | bytes 4718594 | tf_op jit(solution)/shard_map/reduce_sum | solution.py:105
  84.2 7.9 %all-to-all-start.3 = ((bf16[16,384,128]{2,1,0:T(8,128)(2,1)}), bf16[16,384,128]{2,1,0:T(8,128)(2,1)S(1)}, u32[]{:S(2)}, u32[]{:S(2)}) async-start(bf16[16,384,128]{2,1,0:T(8,128)(2,1)} %reduce_sum.21), calls=%async_computation.3 | async-start | bytes 3145728 | tf_op jit(solution)/shard_map/all_to_all | solution.py:106
  92.1 34.2 %all-to-all-done.3 = bf16[16,384,128]{2,1,0:T(8,128)(2,1)S(1)} async-done(((bf16[16,384,128]{2,1,0:T(8,128)(2,1)}), bf16[16,384,128]{2,1,0:T(8,128)(2,1)S(1)}, u32[]{:S(2)}, u32[]{:S(2)}) %all-to-all-start.3) | async-done | bytes 1572896 | tf_op jit(solution)/shard_map/all_to_all | solution.py:106
  126.3 0.2 convert_reduce_fusion
  126.6 0.0 copy-start.4
  126.6 0.0 copy-start.5
  126.7 0.7 divide_subtract_fusion
  127.4 0.7 divide_subtract_fusion.1
  128.2 0.7 divide_subtract_fusion.2
  128.8 0.6 divide_subtract_fusion.3
  (44 shorter events, 0.3 us)
Async XLA Ops:
  0.6 13.2 %copy-start = (bf16[2,19,19,256]{3,0,2,1:T(2,128)(2,1)S(1)}, bf16[2,19,19,256]{3,0,2,1:T(2,128)(2,1)}, u32[]{:S(2)}) copy-start(bf16[2,19,19,256]{3,0,2,1:T(2,128)(2,1)} %param.16) | copy-start | bytes 1108996
  4.0 11.1 %copy-start.18 = (s32[2,2]{1,0:T(2,128)S(1)}, s32[2,2]{1,0:T(2,128)}, u32[]{:S(2)}) copy-start(s32[2,2]{1,0:T(2,128)} %param.17) | copy-start | bytes 52
  4.0 12.1 %copy-start.16 = (s32[2,2]{1,0:T(2,128)S(1)}, s32[2,2]{1,0:T(2,128)}, u32[]{:S(2)}) copy-start(s32[2,2]{1,0:T(2,128)} %param.19) | copy-start | bytes 52
  4.0 12.1 %copy-start.17 = (s32[2,2]{1,0:T(2,128)S(1)}, s32[2,2]{1,0:T(2,128)}, u32[]{:S(2)}) copy-start(s32[2,2]{1,0:T(2,128)} %param.18) | copy-start | bytes 52
  5.5 42.4 %all-to-all-start = ((bf16[16,384,128]{2,1,0:T(8,128)(2,1)}), bf16[16,384,128]{2,1,0:T(8,128)(2,1)S(1)}, u32[]{:S(2)}, u32[]{:S(2)}) async-start(bf16[16,384,128]{2,1,0:T(8,128)(2,1)} %broadcast_in_dim.8), calls=%async_computation | async-start | bytes 3145728 | tf_op jit(solution)/shard_map/all_to_all | solution.py:37
  55.0 1.7 %copy-start.1 = (bf16[2,16,384,128]{3,2,1,0:T(8,128)(2,1)}, bf16[2,16,384,128]{3,2,1,0:T(8,128)(2,1)S(1)}, u32[]{:S(2)}) copy-start(bf16[2,16,384,128]{3,2,1,0:T(8,128)(2,1)S(1)} %all_to_all.20.every) | copy-start | bytes 9437188
  84.1 42.6 %copy-start.2 = (f32[3,3,16,128]{3,2,1,0:T(8,128)S(1)}, f32[3,3,16,128]{3,2,1,0:T(8,128)}, u32[]{:S(2)}) copy-start(f32[3,3,16,128]{3,2,1,0:T(8,128)} %param.21) | copy-start | bytes 221188
  84.1 42.6 %copy-start.7 = (f32[3,3,16,128]{3,2,1,0:T(8,128)S(1)}, f32[3,3,16,128]{3,2,1,0:T(8,128)}, u32[]{:S(2)}) copy-start(f32[3,3,16,128]{3,2,1,0:T(8,128)} %param.26) | copy-start | bytes 221188
  84.1 42.6 %copy-start.8 = (f32[3,3,16,128]{3,2,1,0:T(8,128)S(1)}, f32[3,3,16,128]{3,2,1,0:T(8,128)}, u32[]{:S(2)}) copy-start(f32[3,3,16,128]{3,2,1,0:T(8,128)} %param.27) | copy-start | bytes 221188
  84.1 43.3 %copy-start.3 = (f32[3,3,16,128]{3,2,1,0:T(8,128)S(1)}, f32[3,3,16,128]{3,2,1,0:T(8,128)}, u32[]{:S(2)}) copy-start(f32[3,3,16,128]{3,2,1,0:T(8,128)} %param.20) | copy-start | bytes 221188
  84.1 43.3 %copy-start.9 = (f32[3,3,16,128]{3,2,1,0:T(8,128)S(1)}, f32[3,3,16,128]{3,2,1,0:T(8,128)}, u32[]{:S(2)}) copy-start(f32[3,3,16,128]{3,2,1,0:T(8,128)} %param.24) | copy-start | bytes 221188
  84.1 43.3 %copy-start.10 = (f32[3,3,16,128]{3,2,1,0:T(8,128)S(1)}, f32[3,3,16,128]{3,2,1,0:T(8,128)}, u32[]{:S(2)}) copy-start(f32[3,3,16,128]{3,2,1,0:T(8,128)} %param.25) | copy-start | bytes 221188
  84.1 44.0 %copy-start.6 = (f32[1,16,601]{2,1,0:T(8,128)S(1)}, f32[1,16,601]{2,1,0:T(8,128)}, u32[]{:S(2)}) copy-start(f32[1,16,601]{2,1,0:T(8,128)} %param.22) | copy-start | bytes 115396
  84.1 44.0 %copy-start.11 = (f32[1,16,601]{2,1,0:T(8,128)S(1)}, f32[1,16,601]{2,1,0:T(8,128)}, u32[]{:S(2)}) copy-start(f32[1,16,601]{2,1,0:T(8,128)} %param.28) | copy-start | bytes 115396
  84.1 44.0 %copy-start.12 = (f32[1,16,601]{2,1,0:T(8,128)S(1)}, f32[1,16,601]{2,1,0:T(8,128)}, u32[]{:S(2)}) copy-start(f32[1,16,601]{2,1,0:T(8,128)} %param.29) | copy-start | bytes 115396
  84.2 44.7 %copy-start.13 = (f32[1,16]{1,0:T(1,128)S(1)}, f32[1,16]{1,0:T(1,128)}, u32[]{:S(2)}) copy-start(f32[1,16]{1,0:T(1,128)} %param.23) | copy-start | bytes 196
  84.2 44.7 %copy-start.14 = (f32[1,16]{1,0:T(1,128)S(1)}, f32[1,16]{1,0:T(1,128)}, u32[]{:S(2)}) copy-start(f32[1,16]{1,0:T(1,128)} %param.30) | copy-start | bytes 196
  84.2 44.6 %copy-start.15 = (f32[1,16]{1,0:T(1,128)S(1)}, f32[1,16]{1,0:T(1,128)}, u32[]{:S(2)}) copy-start(f32[1,16]{1,0:T(1,128)} %param.31) | copy-start | bytes 196
  84.2 42.2 %all-to-all-start.3 = ((bf16[16,384,128]{2,1,0:T(8,128)(2,1)}), bf16[16,384,128]{2,1,0:T(8,128)(2,1)S(1)}, u32[]{:S(2)}, u32[]{:S(2)}) async-start(bf16[16,384,128]{2,1,0:T(8,128)(2,1)} %reduce_sum.21), calls=%async_computation.3 | async-start | bytes 3145728 | tf_op jit(solution)/shard_map/all_to_all | solution.py:106
  126.6 2.8 %copy-start.4 = (f32[144,128]{1,0:T(8,128)}, f32[144,128]{1,0:T(8,128)S(1)}, u32[]{:S(2)}) copy-start(f32[144,128]{1,0:T(8,128)S(1)} %get-tuple-element.30) | copy-start | bytes 221188
  126.6 2.8 %copy-start.5 = (f32[144,128]{1,0:T(8,128)}, f32[144,128]{1,0:T(8,128)S(1)}, u32[]{:S(2)}) copy-start(f32[144,128]{1,0:T(8,128)S(1)} %get-tuple-element.31) | copy-start | bytes 221188

commit v2 on v1

--- a/solution.py
+++ b/solution.py
@@ -35,6 +35,10 @@
 def spread(block, axis):
     copies = jnp.broadcast_to(block[None], (lax.axis_size(axis),) + block.shape)
     return lax.all_to_all(copies, axis, 0, 0)
+
+
+def swap_cores(block):
+    return lax.ppermute(block, "mp", [(0, 1), (1, 0)])
 
 
 def row_pad(block, axis):
@@ -61,11 +65,15 @@
             embed.astype(jnp.bfloat16),
         ]
     )
-    everything = spread(spread(packed, "dp"), "mp")
-    embed_used = everything[:, :, -TILE, :rows].reshape(everything.shape[0], CHANNELS)
+    mine = spread(packed, "dp")
+    pair = (mine, swap_cores(mine))
+    lines = [part[:, -TILE, :rows].reshape(CHANNELS) for part in pair]
+    lower = lax.axis_index("mp") == 0
+    embed_used = jnp.stack([jnp.where(lower, *lines), jnp.where(lower, *lines[::-1])])
     if rows != TILE:
-        everything = regroup(everything, rows, blocks)
-    return (everything, embed_used.astype(jnp.float32))
+        both = regroup(jnp.stack(pair), rows, blocks)
+        pair = (both[0], both[1])
+    return (pair, embed_used.astype(jnp.float32))
 
 
 def regroup(everything, rows, blocks):
@@ -101,8 +109,9 @@
     shards = lax.axis_size("dp")
     if rows != TILE:
         packed = ungroup(packed, rows, blocks, shards)
-    halves = lax.all_to_all(packed, "mp", 0, 0)
-    summed = jnp.sum(halves.astype(jnp.float32), axis=0).astype(jnp.bfloat16)
+    arrived = swap_cores(packed[1])
+    summed = packed[0].astype(jnp.float32) + arrived.astype(jnp.float32)
+    summed = summed.astype(jnp.bfloat16)
     owned = lax.all_to_all(summed, "dp", 0, 0)
     total = jnp.sum(owned.astype(jnp.float32), axis=0)
     step = round_up(9 * rows, TILE)
@@ -132,7 +141,9 @@
     passes,
     values,
     rewards,
-    every,
+    place,
+    mine,
+    other,
     states,
     mask,
     embed,
@@ -164,22 +175,27 @@
     cores = CHANNELS // LANES
     groups = CHANNELS // TILE
     spread_cols = blocks * LANES
+    me = place[0]
+
+    def fetch(core, group, at):
+        rows = slice(at, at + TILE)
+        return jnp.where(me == core, mine[group, rows, :], other[group, rows, :])
+
     for core in range(cores):
         lanes = slice(core * LANES, (core + 1) * LANES)
         for group in range(groups):
-            rows = slice(group * TILE, (group + 1) * TILE)
             for tap in range(9):
                 at = tap * CHANNELS + group * TILE
-                first[at : at + TILE, lanes] = every[core, group, tap * TILE : (tap + 1) * TILE, :]
+                first[at : at + TILE, lanes] = fetch(core, group, tap * TILE)
                 two = (9 + tap) * TILE
-                second[at : at + TILE, lanes] = every[core, group, two : two + TILE, :]
+                second[at : at + TILE, lanes] = fetch(core, group, two)
     for which in range(2):
         for group in range(groups):
             for block in range(blocks):
                 at = (18 + block) * TILE
                 head[
                     which, group * TILE : (group + 1) * TILE, block * LANES : (block + 1) * LANES
-                ] = every[which, group, at : at + TILE, :]
+                ] = fetch(which, group, at)
     padded[...] = jnp.zeros(padded.shape, jnp.float32)
     inside = jnp.broadcast_to(mask[...], (extent, CHANNELS)) > 0.5
     cell_at = lax.broadcasted_iota(jnp.int32, (extent, CHANNELS), 0)
@@ -282,8 +298,8 @@
             lanes = slice(core * LANES, (core + 1) * LANES)
             for group in range(groups):
                 rows = slice(group * TILE, (group + 1) * TILE)
-                out[core, group, tap * TILE : (tap + 1) * TILE, :] = one[rows, lanes]
-                out[core, group, (9 + tap) * TILE : (10 + tap) * TILE, :] = two[rows, lanes]
+                out[me ^ core, group, tap * TILE : (tap + 1) * TILE, :] = one[rows, lanes]
+                out[me ^ core, group, (9 + tap) * TILE : (10 + tap) * TILE, :] = two[rows, lanes]
     pooled_bf = pooled_rows.astype(jnp.bfloat16)
     for which in range(2):
         grown = head_scale * tn(pooled_bf, grad_rows[which].astype(jnp.bfloat16))
@@ -297,11 +313,11 @@
             rows = slice(group * TILE, (group + 1) * TILE)
             for block in range(blocks):
                 at = (18 + block) * TILE
-                out[which, group, at : at + TILE, :] = grown[
+                out[me ^ which, group, at : at + TILE, :] = grown[
                     rows, block * LANES : (block + 1) * LANES
                 ]
             at = (18 + blocks) * TILE
-            out[which, group, at : at + TILE, :] = line
+            out[me ^ which, group, at : at + TILE, :] = line
 
 
 def window(every, embed, states, moves, values, rewards, buckets, total):
@@ -330,12 +346,13 @@
         blocks=blocks,
         total=total,
     )
+    place = lax.axis_index("mp").reshape(1)
     smem = pl.BlockSpec(memory_space=pltpu.SMEM)
     vmem = pl.BlockSpec(memory_space=pltpu.VMEM)
     return pl.pallas_call(
         body,
-        out_shape=jax.ShapeDtypeStruct(every.shape, jnp.bfloat16),
-        in_specs=[smem] * 4 + [vmem] * 4,
+        out_shape=jax.ShapeDtypeStruct((2,) + every[0].shape, jnp.bfloat16),
+        in_specs=[smem] * 5 + [vmem] * 5,
         out_specs=vmem,
         scratch_shapes=[
             pltpu.VMEM((9 * CHANNELS, CHANNELS), jnp.bfloat16),
@@ -351,7 +368,7 @@
             pltpu.VMEM((deep, CHANNELS), jnp.bfloat16),
         ],
         compiler_params=pltpu.CompilerParams(vmem_limit_bytes=56 * 1024 * 1024),
-    )(spots, passes, values, rewards, every, states, mask, embed)
+    )(spots, passes, values, rewards, place, *every, states, mask, embed)
 
 
 def local(

time: 132 us -> 123 us (0.932)
  blocking collectives: 13.8 us -> 45.7 us
  waiting for transfers between devices: 64.7 us -> 37.1 us
  starting transfers between devices: 16.2 us -> 4.56 us
  local copies, waits for them, and re-layouts: 5.68 us -> 4.2 us
    all_to_all x1, blocking collectives: 6.26 us -> 45.7 us  [spread(): return lax.all_to_all(copies, axis, 0, 0)]
    all_to_all x1 -> x0, waiting for transfers between devices: 30.5 us -> none  [spread(): return lax.all_to_all(copies, axis, 0, 0)]
    all_to_all x1 -> x0, starting transfers between devices: 8.34 us -> none  [spread(): return lax.all_to_all(copies, axis, 0, 0)]
    all_to_all x1 -> x0, blocking collectives: 7.55 us -> none  [scatter_grads(): halves = lax.all_to_all(packed, 'mp', 0, 0)]
    all_to_all x1, starting transfers between devices: 7.89 us -> 3.95 us  [scatter_grads(): owned = lax.all_to_all(summed, 'dp', 0, 0)]
    ppermute x0 -> x2, waiting for transfers between devices: none -> 3.04 us  [swap_cores(): return lax.ppermute(block, 'mp', [(0, 1), (1, 0)])]
    convert_element_type x1 -> x2, other arithmetic: 0.05 us -> 2.36 us  [the longest x1 1.57 us: scatter_grads(): summed = summed.astype(jnp.bfloat16)]
    reduce_sum x1 -> x0, other arithmetic: 2.21 us -> none  [scatter_grads(): summed = jnp.sum(halves.astype(jnp.float32), axis=0).astype(jnp.bfloat16)]
  transfers between devices with their start and end apart: 2 -> 3, of which waited for: 2 -> 2; matrix products, arithmetic and copies ran while one was open for 3% -> 3% of each run, Pallas kernels for 0% -> 0%
where the time goes in v2:
time: 123 us; the launch traced here: 121 us
  blocking collectives  45.7 us (37%)
  waiting for transfers between devices  37.1 us (30%)
  Pallas kernels  17.9 us (15%)
  other arithmetic  10.5 us (9%)
  starting transfers between devices  4.56 us (4%)
  local copies, waits for them, and re-layouts  4.2 us (3%)
    all_to_all x1, blocking collectives, spread(): return lax.all_to_all(copies, axis, 0, 0)  45.7 us
    all_to_all x1, waiting for transfers between devices, scatter_grads(): owned = lax.all_to_all(summed, 'dp', 0, 0)  34.1 us
    pallas_call x1, Pallas kernels, window(): pl.pallas_call(body, out_shape=jax.ShapeDtypeStruct((2,) + every[0].shape...  17.9 us
    all_to_all x1, starting transfers between devices, scatter_grads(): owned = lax.all_to_all(summed, 'dp', 0, 0)  3.95 us
    ppermute x2, waiting for transfers between devices, swap_cores(): return lax.ppermute(block, 'mp', [(0, 1), (1, 0)])  3.04 us
    sub x4, other arithmetic, adam_update(): param_new = param - step_size * mean_new / (jnp.sqrt(square_new) + eps_adam)  2.69 us
  transfers between devices with their start and end apart: 3, of which 2 were waited for; matrix products, arithmetic and copies ran while one was open for 3% of the time, Pallas kernels for 0%

profile of v2, /device:TPU:0, one launch (start us, length us, event | category | flops | bytes accessed | tf_op | source)
XLA Modules:
  0.0 121.1 jit_solution(13998796248281684745)
XLA Ops:
  0.6 0.0 copy-start
  0.7 0.7 convert.11
  1.4 0.8 convert_bitcast_fusion
  2.2 0.9 convert_element_type.54
  3.1 0.9 convert_element_type.55
  4.0 0.3 broadcast_in_dim.12
  4.3 45.7 %all_to_all.10.mine = bf16[16,384,128]{2,1,0:T(8,128)(2,1)S(1)} all-to-all(bf16[16,384,128]{2,1,0:T(8,128)(2,1)S(1)} %broadcast_in_dim.12), channel_id=1, replica_groups=mesh['dp'=16,'mp'=2] {'dp'}, dimensions={0} | all-to-all | bytes 3145728 | tf_op jit(solution)/shard_map/all_to_all | solution.py:37
  50.0 0.1 collective-permute-start
  50.1 0.4 constant_dynamic-slice_fusion.1
  50.6 0.7 pad.21.states
  51.3 0.5 compare_convert_fusion.passes
  51.8 0.5 compare_select_fusion.spots
  52.4 0.5 constant_dynamic-slice_fusion.2
  52.9 0.8 fusion.11.mask
  53.7 0.1 fusion.17
  53.8 0.1 select_n.90
  53.9 0.1 select_n.92
  54.0 0.8 maximum_convert_fusion.embed
  54.7 0.2 copy-done.3
  54.9 17.9 %shard_map.279 = bf16[2,16,384,128]{3,2,1,0:T(8,128)(2,1)} custom-call(s32[1,2]{1,0:T(1,128)} %compare_select_fusion.spots, s32[1,2]{1,0:T(1,128)} %compare_convert_fusion.passes, s32[1,2]{1,0:T(1,128)} %get-tuple-element.35.values, s32[1,2]{1,0:T(1,128)} %get-tuple-element.34.rewards, s32[1]{0:T(128)} %bitcast.place, bf16[16,384,128]{2,1,0:T(8,128)(2,1)} %copy-done.2, ...), custom_call_target="tpu_custom_call" | custom-call | tf_op jit(solution)/shard_map/pallas_call | solution.py:352
  72.8 1.7 %slice_bitcast_fusion = bf16[16,384,128]{2,1,0:T(8,128)(2,1)S(1)} fusion(bf16[2,16,384,128]{3,2,1,0:T(8,128)(2,1)} %shard_map.279), kind=kLoop, calls=%fused_computation.3 | loop fusion | bytes 3145728 | tf_op jit(solution)/shard_map/squeeze | solution.py:112
  74.5 0.5 collective-permute-start.1
  75.0 3.0 %collective-permute-done.1 = bf16[16,384,128]{2,1,0:T(8,128)(2,1)S(1)} collective-permute-done((bf16[16,384,128]{2,1,0:T(8,128)(2,1)S(1)}, bf16[16,384,128]{2,1,0:T(8,128)(2,1)S(1)}, u32[]{:S(2)}, u32[]{:S(2)}) %collective-permute-start.1) | collective-permute-done | bytes 1572896 | tf_op jit(solution)/shard_map/ppermute | solution.py:41
  78.0 1.6 %fusion = bf16[16,384,128]{2,1,0:T(8,128)(2,1)} fusion(bf16[16,384,128]{2,1,0:T(8,128)(2,1)S(1)} %collective-permute-done.1, bf16[2,16,384,128]{3,2,1,0:T(8,128)(2,1)S(1)} %copy-done.1), kind=kLoop, calls=%fused_computation.1 | loop fusion | flops 3145728 | bytes 4718592 | tf_op jit(solution)/shard_map/convert_element_type | solution.py:114
  79.6 3.9 %all-to-all-start.1 = ((bf16[16,384,128]{2,1,0:T(8,128)(2,1)}), bf16[16,384,128]{2,1,0:T(8,128)(2,1)S(1)}, u32[]{:S(2)}, u32[]{:S(2)}) async-start(bf16[16,384,128]{2,1,0:T(8,128)(2,1)} %fusion), calls=%async_computation.1 | async-start | bytes 3145728 | tf_op jit(solution)/shard_map/all_to_all | solution.py:115
  83.7 34.1 %all-to-all-done.1 = bf16[16,384,128]{2,1,0:T(8,128)(2,1)S(1)} async-done(((bf16[16,384,128]{2,1,0:T(8,128)(2,1)}), bf16[16,384,128]{2,1,0:T(8,128)(2,1)S(1)}, u32[]{:S(2)}, u32[]{:S(2)}) %all-to-all-start.1) | async-done | bytes 1572896 | tf_op jit(solution)/shard_map/all_to_all | solution.py:115
  117.8 0.2 convert_reduce_fusion
  118.1 0.0 copy-start.6
  118.2 0.7 divide_subtract_fusion.2
  118.9 0.7 divide_subtract_fusion.1
  119.6 0.7 divide_subtract_fusion
  120.3 0.6 divide_subtract_fusion.3
  (51 shorter events, 0.3 us)
Async XLA Ops:
  0.6 49.5 %copy-start = (bf16[2,19,19,256]{3,0,2,1:T(2,128)(2,1)S(1)}, bf16[2,19,19,256]{3,0,2,1:T(2,128)(2,1)}, u32[]{:S(2)}) copy-start(bf16[2,19,19,256]{3,0,2,1:T(2,128)(2,1)} %param.16) | copy-start | bytes 1108996
  50.0 4.7 %copy-start.2 = (bf16[16,384,128]{2,1,0:T(8,128)(2,1)}, bf16[16,384,128]{2,1,0:T(8,128)(2,1)S(1)}, u32[]{:S(2)}) copy-start(bf16[16,384,128]{2,1,0:T(8,128)(2,1)S(1)} %all_to_all.10.mine) | copy-start | bytes 4718596
  50.0 1.3 %copy-start.20 = (s32[2,2]{1,0:T(2,128)S(1)}, s32[2,2]{1,0:T(2,128)}, u32[]{:S(2)}) copy-start(s32[2,2]{1,0:T(2,128)} %param.17) | copy-start | bytes 52
  50.0 2.3 %copy-start.18 = (s32[2,2]{1,0:T(2,128)S(1)}, s32[2,2]{1,0:T(2,128)}, u32[]{:S(2)}) copy-start(s32[2,2]{1,0:T(2,128)} %param.19) | copy-start | bytes 52
  50.0 2.3 %copy-start.19 = (s32[2,2]{1,0:T(2,128)S(1)}, s32[2,2]{1,0:T(2,128)}, u32[]{:S(2)}) copy-start(s32[2,2]{1,0:T(2,128)} %param.18) | copy-start | bytes 52
  50.0 3.7 %collective-permute-start = (bf16[16,384,128]{2,1,0:T(8,128)(2,1)S(1)}, bf16[16,384,128]{2,1,0:T(8,128)(2,1)S(1)}, u32[]{:S(2)}, u32[]{:S(2)}) collective-permute-start(bf16[16,384,128]{2,1,0:T(8,128)(2,1)S(1)} %all_to_all.10.mine), channel_id=1, source_target_pairs={{0,1},{1,0},{2,3},{3,2},{4,5},{5,4},{6,7},{7,6},{8,9},{9,8},{10,11... | collective-permute-start | bytes 4718600 | tf_op jit(solution)/shard_map/ppermute | solution.py:41
  53.7 1.2 copy-start.3
  72.8 5.3 %copy-start.1 = (bf16[2,16,384,128]{3,2,1,0:T(8,128)(2,1)S(1)}, bf16[2,16,384,128]{3,2,1,0:T(8,128)(2,1)}, u32[]{:S(2)}) copy-start(bf16[2,16,384,128]{3,2,1,0:T(8,128)(2,1)} %shard_map.279) | copy-start | bytes 9437188
  74.5 3.6 %collective-permute-start.1 = (bf16[16,384,128]{2,1,0:T(8,128)(2,1)S(1)}, bf16[16,384,128]{2,1,0:T(8,128)(2,1)S(1)}, u32[]{:S(2)}, u32[]{:S(2)}) collective-permute-start(bf16[16,384,128]{2,1,0:T(8,128)(2,1)S(1)} %slice_bitcast_fusion), channel_id=1, source_target_pairs={{0,1},{1,0},{2,3},{3,2},{4,5},{5,4},{6,7},{7,6},{8,9},{9,8},{10,11... | collective-permute-start | bytes 4718600 | tf_op jit(solution)/shard_map/ppermute | solution.py:41
  79.6 38.2 %all-to-all-start.1 = ((bf16[16,384,128]{2,1,0:T(8,128)(2,1)}), bf16[16,384,128]{2,1,0:T(8,128)(2,1)S(1)}, u32[]{:S(2)}, u32[]{:S(2)}) async-start(bf16[16,384,128]{2,1,0:T(8,128)(2,1)} %fusion), calls=%async_computation.1 | async-start | bytes 3145728 | tf_op jit(solution)/shard_map/all_to_all | solution.py:115
  83.6 34.6 %copy-start.8 = (f32[1,16,601]{2,1,0:T(8,128)S(1)}, f32[1,16,601]{2,1,0:T(8,128)}, u32[]{:S(2)}) copy-start(f32[1,16,601]{2,1,0:T(8,128)} %param.22) | copy-start | bytes 115396
  83.6 34.6 %copy-start.13 = (f32[1,16,601]{2,1,0:T(8,128)S(1)}, f32[1,16,601]{2,1,0:T(8,128)}, u32[]{:S(2)}) copy-start(f32[1,16,601]{2,1,0:T(8,128)} %param.28) | copy-start | bytes 115396
  83.6 34.6 %copy-start.14 = (f32[1,16,601]{2,1,0:T(8,128)S(1)}, f32[1,16,601]{2,1,0:T(8,128)}, u32[]{:S(2)}) copy-start(f32[1,16,601]{2,1,0:T(8,128)} %param.29) | copy-start | bytes 115396
  83.6 35.3 %copy-start.4 = (f32[3,3,16,128]{3,2,1,0:T(8,128)S(1)}, f32[3,3,16,128]{3,2,1,0:T(8,128)}, u32[]{:S(2)}) copy-start(f32[3,3,16,128]{3,2,1,0:T(8,128)} %param.20) | copy-start | bytes 221188
  83.6 35.2 %copy-start.9 = (f32[3,3,16,128]{3,2,1,0:T(8,128)S(1)}, f32[3,3,16,128]{3,2,1,0:T(8,128)}, u32[]{:S(2)}) copy-start(f32[3,3,16,128]{3,2,1,0:T(8,128)} %param.24) | copy-start | bytes 221188
  83.6 35.2 %copy-start.10 = (f32[3,3,16,128]{3,2,1,0:T(8,128)S(1)}, f32[3,3,16,128]{3,2,1,0:T(8,128)}, u32[]{:S(2)}) copy-start(f32[3,3,16,128]{3,2,1,0:T(8,128)} %param.25) | copy-start | bytes 221188
  83.6 35.9 %copy-start.5 = (f32[3,3,16,128]{3,2,1,0:T(8,128)S(1)}, f32[3,3,16,128]{3,2,1,0:T(8,128)}, u32[]{:S(2)}) copy-start(f32[3,3,16,128]{3,2,1,0:T(8,128)} %param.21) | copy-start | bytes 221188
  83.7 35.9 %copy-start.11 = (f32[3,3,16,128]{3,2,1,0:T(8,128)S(1)}, f32[3,3,16,128]{3,2,1,0:T(8,128)}, u32[]{:S(2)}) copy-start(f32[3,3,16,128]{3,2,1,0:T(8,128)} %param.26) | copy-start | bytes 221188
  83.7 35.9 %copy-start.12 = (f32[3,3,16,128]{3,2,1,0:T(8,128)S(1)}, f32[3,3,16,128]{3,2,1,0:T(8,128)}, u32[]{:S(2)}) copy-start(f32[3,3,16,128]{3,2,1,0:T(8,128)} %param.27) | copy-start | bytes 221188
  83.7 36.6 %copy-start.15 = (f32[1,16]{1,0:T(1,128)S(1)}, f32[1,16]{1,0:T(1,128)}, u32[]{:S(2)}) copy-start(f32[1,16]{1,0:T(1,128)} %param.23) | copy-start | bytes 196
  83.7 36.6 %copy-start.16 = (f32[1,16]{1,0:T(1,128)S(1)}, f32[1,16]{1,0:T(1,128)}, u32[]{:S(2)}) copy-start(f32[1,16]{1,0:T(1,128)} %param.30) | copy-start | bytes 196
  83.7 36.6 %copy-start.17 = (f32[1,16]{1,0:T(1,128)S(1)}, f32[1,16]{1,0:T(1,128)}, u32[]{:S(2)}) copy-start(f32[1,16]{1,0:T(1,128)} %param.31) | copy-start | bytes 196
  118.1 2.8 %copy-start.6 = (f32[144,128]{1,0:T(8,128)}, f32[144,128]{1,0:T(8,128)S(1)}, u32[]{:S(2)}) copy-start(f32[144,128]{1,0:T(8,128)S(1)} %get-tuple-element.32) | copy-start | bytes 221188
  118.1 2.8 %copy-start.7 = (f32[144,128]{1,0:T(8,128)}, f32[144,128]{1,0:T(8,128)S(1)}, u32[]{:S(2)}) copy-start(f32[144,128]{1,0:T(8,128)S(1)} %get-tuple-element.33) | copy-start | bytes 221188
